TPU v7x, 128 devices: a whole 4x4x4 slice. The times are simulated.
128 devices in a mesh: batch: 16 (over y, x), cols: 8 (over z, core).
Axes of the slice: x: 4, y: 4, z: 4, core: 2. Of those that a mesh axis runs over, the one named last changes fastest.
Arguments:
- grad_up: float32 [16, 1024, 4096], P('batch', None, 'cols'), may hold values from -0.875 to 0.875
- grad_down: float32 [16, 4096, 1024], P('batch', 'cols'), may hold values from -0.875 to 0.875
- grad_query: float32 [16, 1024, 1024], P('batch', None, 'cols'), may hold values from -0.875 to 0.875
- grad_key: float32 [16, 1024, 1024], P('batch', None, 'cols'), may hold values from -0.875 to 0.875
- grad_value: float32 [16, 1024, 1024], P('batch', None, 'cols'), may hold values from -0.875 to 0.875
- grad_mixed: float32 [16, 1024, 1024], P('batch', 'cols'), may hold values from -0.875 to 0.875
- grad_norm: float32 [16, 1024], P('batch'), may hold values from -8 to 8
- weight_up: float32 [1024, 4096], P('batch', 'cols'), may hold values from -0.1875 to 0.1875
- weight_down: float32 [4096, 1024], P('cols', 'batch'), may hold values from -0.09375 to 0.09375
- weight_query: float32 [1024, 1024], P('batch', 'cols'), may hold values from -0.1875 to 0.1875
- weight_key: float32 [1024, 1024], P('batch', 'cols'), may hold values from -0.1875 to 0.1875
- weight_value: float32 [1024, 1024], P('batch', 'cols'), may hold values from -0.1875 to 0.1875
- weight_mixed: float32 [1024, 1024], P('cols', 'batch'), may hold values from -0.1875 to 0.1875
- weight_norm: float32 [1024], P('batch'), may hold values from 0.25 to 1.75
- moment_up: float32 [1024, 4096], P('batch', 'cols'), may hold values from -1.75 to 1.75
- moment_down: float32 [4096, 1024], P('cols', 'batch'), may hold values from -1.75 to 1.75
- moment_query: float32 [1024, 1024], P('batch', 'cols'), may hold values from -1.75 to 1.75
- moment_key: float32 [1024, 1024], P('batch', 'cols'), may hold values from -1.75 to 1.75
- moment_value: float32 [1024, 1024], P('batch', 'cols'), may hold values from -1.75 to 1.75
- moment_mixed: float32 [1024, 1024], P('cols', 'batch'), may hold values from -1.75 to 1.75
- moment_norm: float32 [1024], P('batch'), may hold values from -1.75 to 1.75
Outputs:
- copy_up: bfloat16 [1024, 4096], P(None, 'cols')
- copy_down: bfloat16 [4096, 1024], P('cols')
- copy_query: bfloat16 [1024, 1024], P(None, 'cols')
- copy_key: bfloat16 [1024, 1024], P(None, 'cols')
- copy_value: bfloat16 [1024, 1024], P(None, 'cols')
- copy_mixed: bfloat16 [1024, 1024], P('cols')
- copy_norm: bfloat16 [1024], replicated
- new_up: float32 [1024, 4096], P('batch', 'cols')
- new_down: float32 [4096, 1024], P('cols', 'batch')
- new_query: float32 [1024, 1024], P('batch', 'cols')
- new_key: float32 [1024, 1024], P('batch', 'cols')
- new_value: float32 [1024, 1024], P('batch', 'cols')
- new_mixed: float32 [1024, 1024], P('cols', 'batch')
- new_norm: float32 [1024], P('batch')
- state_new_up: float32 [1024, 4096], P('batch', 'cols')
- state_new_down: float32 [4096, 1024], P('cols', 'batch')
- state_new_query: float32 [1024, 1024], P('batch', 'cols')
- state_new_key: float32 [1024, 1024], P('batch', 'cols')
- state_new_value: float32 [1024, 1024], P('batch', 'cols')
- state_new_mixed: float32 [1024, 1024], P('cols', 'batch')
- state_new_norm: float32 [1024], P('batch')
All inputs are finite; a program needn't handle non-finite values.
Results may differ from a plain program's by a relative error of at most 0.008.
Values may be sent and summed in bfloat16 or wider, within the bound.
A program may use at most 64 MiB of HBM per device.

v0:
```python
import jax
import jax.numpy as jnp
from jax import lax
from jax.sharding import PartitionSpec as P

learn_rate = 0.1
hold_rate = 0.7


def cut_along(value, dim, devices):
    before, after = (value.shape[:dim], value.shape[dim + 1 :])
    return jnp.moveaxis(value.reshape(*before, devices, -1, *after), dim, 0)


def sum_packed(arrays, axis, dims):
    devices = lax.axis_size(axis)
    tiles = [cut_along(a, dim, devices) for a, dim in zip(arrays, dims)]
    lines = jnp.concatenate([b.reshape(devices, -1) for b in tiles], axis=1)
    span = max(16, -(-lines.shape[1] // 1024) * 8)
    lines = jnp.pad(lines, ((0, 0), (0, span * 128 - lines.shape[1]))).reshape(-1, 128)
    line, at, outs = (lax.psum_scatter(lines, axis, tiled=True).reshape(-1), 0, [])
    for b in tiles:
        part = b[0]
        outs.append(line[at : at + part.size].reshape(part.shape))
        at += part.size
    return tuple(outs)


def rows_first(arrays, axis, dims):
    turned = [jnp.moveaxis(a, dim, 0) for a, dim in zip(arrays, dims)]
    widths = [t[0].size for t in turned]
    both = jnp.concatenate([t.reshape(-1, w) for t, w in zip(turned, widths)], axis=1)
    filled = lax.all_gather(both, axis, axis=0, tiled=True)
    tiles = jnp.split(filled, [sum(widths[:k]) for k in range(1, len(widths))], axis=1)
    return tuple(
        (
            jnp.moveaxis(b.reshape(-1, *t.shape[1:]), 0, dim)
            for b, t, dim in zip(tiles, turned, dims)
        )
    )


def body(
    grad_up,
    grad_down,
    grad_query,
    grad_key,
    grad_value,
    grad_mixed,
    grad_norm,
    weight_up,
    weight_down,
    weight_query,
    weight_key,
    weight_value,
    weight_mixed,
    weight_norm,
    moment_up,
    moment_down,
    moment_query,
    moment_key,
    moment_value,
    moment_mixed,
    moment_norm,
):
    mean_up, mean_down, mean_query, mean_key, mean_value, mean_mixed, mean_norm = sum_packed(
        (
            grad_up[0],
            grad_down[0],
            grad_query[0],
            grad_key[0],
            grad_value[0],
            grad_mixed[0],
            grad_norm[0],
        ),
        "batch",
        (0, 1, 0, 0, 0, 1, 0),
    )
    mean_rate = lax.axis_size("batch") ** (-0.5)
    mean_up = mean_up * mean_rate
    mean_down = mean_down * mean_rate
    mean_query = mean_query * mean_rate
    mean_key = mean_key * mean_rate
    mean_value = mean_value * mean_rate
    mean_mixed = mean_mixed * mean_rate
    mean_norm = mean_norm * mean_rate
    state_new_up = hold_rate * moment_up + mean_up
    new_up = weight_up - learn_rate * state_new_up
    state_new_down = hold_rate * moment_down + mean_down
    new_down = weight_down - learn_rate * state_new_down
    state_new_query = hold_rate * moment_query + mean_query
    new_query = weight_query - learn_rate * state_new_query
    state_new_key = hold_rate * moment_key + mean_key
    new_key = weight_key - learn_rate * state_new_key
    state_new_value = hold_rate * moment_value + mean_value
    new_value = weight_value - learn_rate * state_new_value
    state_new_mixed = hold_rate * moment_mixed + mean_mixed
    new_mixed = weight_mixed - learn_rate * state_new_mixed
    state_new_norm = hold_rate * moment_norm + mean_norm
    new_norm = weight_norm - learn_rate * state_new_norm
    copy_up, copy_down, copy_query, copy_key, copy_value, copy_mixed, copy_norm = rows_first(
        (
            new_up.astype(jnp.bfloat16),
            new_down.astype(jnp.bfloat16),
            new_query.astype(jnp.bfloat16),
            new_key.astype(jnp.bfloat16),
            new_value.astype(jnp.bfloat16),
            new_mixed.astype(jnp.bfloat16),
            new_norm.astype(jnp.bfloat16),
        ),
        "batch",
        (0, 1, 0, 0, 0, 1, 0),
    )
    return (
        copy_up,
        copy_down,
        copy_query,
        copy_key,
        copy_value,
        copy_mixed,
        copy_norm,
        new_up,
        new_down,
        new_query,
        new_key,
        new_value,
        new_mixed,
        new_norm,
        state_new_up,
        state_new_down,
        state_new_query,
        state_new_key,
        state_new_value,
        state_new_mixed,
        state_new_norm,
    )


def solution(mesh):
    in_specs = (
        P("batch", None, "cols"),
        P("batch", "cols", None),
        P("batch", None, "cols"),
        P("batch", None, "cols"),
        P("batch", None, "cols"),
        P("batch", "cols", None),
        P("batch", None),
        P("batch", "cols"),
        P("cols", "batch"),
        P("batch", "cols"),
        P("batch", "cols"),
        P("batch", "cols"),
        P("cols", "batch"),
        P("batch"),
        P("batch", "cols"),
        P("cols", "batch"),
        P("batch", "cols"),
        P("batch", "cols"),
        P("batch", "cols"),
        P("cols", "batch"),
        P("batch"),
    )
    out_specs = (
        P(None, "cols"),
        P("cols", None),
        P(None, "cols"),
        P(None, "cols"),
        P(None, "cols"),
        P("cols", None),
        P(),
        P("batch", "cols"),
        P("cols", "batch"),
        P("batch", "cols"),
        P("batch", "cols"),
        P("batch", "cols"),
        P("cols", "batch"),
        P("batch"),
        P("batch", "cols"),
        P("cols", "batch"),
        P("batch", "cols"),
        P("batch", "cols"),
        P("batch", "cols"),
        P("cols", "batch"),
        P("batch"),
    )
    return jax.shard_map(body, mesh=mesh, in_specs=in_specs, out_specs=out_specs, check_vma=False)
```

profile of v0, /device:TPU:0, one launch (start us, length us, event | category | flops | bytes accessed | tf_op | source)
XLA Modules:
  0.0 246.3 jit_solution(13015991493794930833)
XLA Ops:
  7.2 1.8 reshape_reshape_squeeze.12
  9.0 1.5 constant_dynamic-update-slice_fusion.6
  10.5 1.9 copy.92
  12.5 2.7 %copy.93 = f32[16,512,64]{2,1,0:T(8,128)} copy(f32[16,512,64]{1,2,0:T(8,128)S(1)} %bitcast.19) | data formatting | bytes 4194304 | tf_op jit(solution)/shard_map/transpose | solution.py:12
  15.2 2.9 %reshape.84 = f32[16,32768]{1,0:T(8,128)S(1)} reshape(f32[16,512,64]{2,1,0:T(8,128)} %copy.93) | data formatting | bytes 4194304 | tf_op jit(solution)/shard_map/reshape | solution.py:18
  19.9 1.9 reshape_reshape_squeeze.15
  21.9 2.1 copy.94
  23.9 1.4 copy.95
  25.3 1.2 reshape.85
  27.7 1.4 constant_dynamic-update-slice_fusion.5
  29.2 1.9 constant_dynamic-update-slice_fusion.4
  31.1 1.9 constant_dynamic-update-slice_fusion.3
  35.3 5.8 %pad.4 = f32[16,99328]{1,0:T(8,128)} pad(f32[16,98368]{1,0:T(8,128)} %constant_dynamic-update-slice_fusion, f32[]{:T(128)} %constant.5.clone.1), padding=0_0x0_960 | pad | bytes 12652548 | tf_op jit(solution)/shard_map/jit(_pad)/pad | solution.py:20
  41.1 5.0 %reshape.86 = f32[12416,128]{1,0:T(8,128)} reshape(f32[16,99328]{1,0:T(8,128)} %pad.4) | data formatting | bytes 12713984 | tf_op jit(solution)/shard_map/reshape | solution.py:20
  48.0 123.4 %all-reduce.4.cloned.1.call-done = f32[12416,128]{1,0:T(8,128)} async-done(((f32[12416,128]{1,0:T(8,128)}), f32[12416,128]{1,0:T(8,128)}) %all-reduce.4.cloned.1.call-update) | async-done | bytes 6357008
  173.6 1.0 dynamic-slice_bitcast_fusion
  176.8 1.4 constant_dynamic-update-slice_fusion.11
  178.2 1.4 constant_dynamic-update-slice_fusion.10
  179.6 1.4 constant_dynamic-update-slice_fusion.9
  182.4 48.5 %all-gather.2.cloned.1.call-done = bf16[1024,1537]{1,0:T(8,128)(2,1)} async-done(((bf16[64,1537]{1,0:T(8,128)(2,1)}), bf16[1024,1537]{1,0:T(8,128)(2,1)}) %all-gather.2.cloned.1.call-update) | async-done | bytes 3147792 | tf_op jit(solution)/shard_map/all_gather | solution.py:33
  230.9 2.7 %slice_bitcast_fusion = (bf16[512,1024]{0,1:T(8,128)(2,1)S(1)}, bf16[1024,512]{1,0:T(8,128)(2,1)}) fusion(bf16[1024,1537]{1,0:T(8,128)(2,1)} %all-gather.2.cloned.1.call-done), kind=kLoop, calls=%fused_computation | loop fusion | bytes 4194304 | tf_op jit(solution)/shard_map/transpose | solution.py:37
  233.5 1.3 copy.99
  234.9 2.1 slice_bitcast_fusion.1
  237.8 1.7 slice_reduce_fusion
  (69 shorter events, 13.0 us)
Async XLA Ops:
  7.2 164.3 %all-reduce.4.cloned.1.call-start = ((), (), s32[]{:S(2)}) async-start(), calls=%async_computation.1 | async-start | bytes 12713984
  12.5 5.7 %copy-start.2 = (f32[1,1024,128]{2,1,0:T(8,128)S(1)}, f32[1,1024,128]{2,1,0:T(8,128)}, u32[]{:S(2)}) copy-start(f32[1,1024,128]{2,1,0:T(8,128)} %param.23) | copy-start | bytes 1572868
  12.5 6.6 %copy-start.3 = (f32[1,1024,128]{2,1,0:T(8,128)S(1)}, f32[1,1024,128]{2,1,0:T(8,128)}, u32[]{:S(2)}) copy-start(f32[1,1024,128]{2,1,0:T(8,128)} %param.24) | copy-start | bytes 1572868
  15.2 11.8 %copy-start.17 = (f32[1,1024]{1,0:T(1,128)S(1)}, f32[1,1024]{1,0:T(1,128)}, u32[]{:S(2)}) copy-start(f32[1,1024]{1,0:T(1,128)} %param.27) | copy-start | bytes 12292
  26.5 6.5 %copy-start.1 = (f32[16,8192]{1,0:T(8,128)S(1)}, f32[16,8192]{1,0:T(8,128)}, u32[]{:S(2)}) copy-start(f32[16,8192]{1,0:T(8,128)} %reshape_reshape_squeeze.15) | copy-start | bytes 1572868
  26.5 7.3 %copy-start = (f32[16,8192]{1,0:T(8,128)S(1)}, f32[16,8192]{1,0:T(8,128)}, u32[]{:S(2)}) copy-start(f32[16,8192]{1,0:T(8,128)} %reshape.85) | copy-start | bytes 1572868
  46.2 0.7 copy-start.20
  46.2 128.5 %copy-start.18 = (f32[64]{0:T(128)S(1)}, f32[64]{0:T(128)}, u32[]{:S(2)}) copy-start(f32[64]{0:T(128)} %param.34) | copy-start | bytes 772
  46.2 128.5 %copy-start.19 = (f32[64]{0:T(128)S(1)}, f32[64]{0:T(128)}, u32[]{:S(2)}) copy-start(f32[64]{0:T(128)} %param.41) | copy-start | bytes 772
  46.2 129.2 %copy-start.5 = (f32[64,512]{1,0:T(8,128)S(1)}, f32[64,512]{1,0:T(8,128)}, u32[]{:S(2)}) copy-start(f32[64,512]{1,0:T(8,128)} %param.28) | copy-start | bytes 393220
  46.2 129.2 %copy-start.6 = (f32[64,512]{1,0:T(8,128)S(1)}, f32[64,512]{1,0:T(8,128)}, u32[]{:S(2)}) copy-start(f32[64,512]{1,0:T(8,128)} %param.35) | copy-start | bytes 393220
  46.2 129.9 %copy-start.7 = (f32[512,64]{0,1:T(8,128)S(1)}, f32[512,64]{0,1:T(8,128)}, u32[]{:S(2)}) copy-start(f32[512,64]{0,1:T(8,128)} %param.29) | copy-start | bytes 393220
  46.2 129.9 %copy-start.8 = (f32[512,64]{0,1:T(8,128)S(1)}, f32[512,64]{0,1:T(8,128)}, u32[]{:S(2)}) copy-start(f32[512,64]{0,1:T(8,128)} %param.36) | copy-start | bytes 393220
  46.2 130.6 %copy-start.9 = (f32[64,128]{1,0:T(8,128)S(1)}, f32[64,128]{1,0:T(8,128)}, u32[]{:S(2)}) copy-start(f32[64,128]{1,0:T(8,128)} %param.30) | copy-start | bytes 98308
  46.2 130.6 %copy-start.10 = (f32[64,128]{1,0:T(8,128)S(1)}, f32[64,128]{1,0:T(8,128)}, u32[]{:S(2)}) copy-start(f32[64,128]{1,0:T(8,128)} %param.37) | copy-start | bytes 98308
  46.2 132.0 %copy-start.11 = (f32[64,128]{1,0:T(8,128)S(1)}, f32[64,128]{1,0:T(8,128)}, u32[]{:S(2)}) copy-start(f32[64,128]{1,0:T(8,128)} %param.31) | copy-start | bytes 98308
  46.2 132.0 %copy-start.12 = (f32[64,128]{1,0:T(8,128)S(1)}, f32[64,128]{1,0:T(8,128)}, u32[]{:S(2)}) copy-start(f32[64,128]{1,0:T(8,128)} %param.38) | copy-start | bytes 98308
  46.3 133.4 %copy-start.13 = (f32[64,128]{1,0:T(8,128)S(1)}, f32[64,128]{1,0:T(8,128)}, u32[]{:S(2)}) copy-start(f32[64,128]{1,0:T(8,128)} %param.32) | copy-start | bytes 98308
  46.3 133.4 %copy-start.14 = (f32[64,128]{1,0:T(8,128)S(1)}, f32[64,128]{1,0:T(8,128)}, u32[]{:S(2)}) copy-start(f32[64,128]{1,0:T(8,128)} %param.39) | copy-start | bytes 98308
  46.3 134.8 %copy-start.15 = (f32[128,64]{0,1:T(8,128)S(1)}, f32[128,64]{0,1:T(8,128)}, u32[]{:S(2)}) copy-start(f32[128,64]{0,1:T(8,128)} %param.33) | copy-start | bytes 98308
  46.3 134.8 %copy-start.16 = (f32[128,64]{0,1:T(8,128)S(1)}, f32[128,64]{0,1:T(8,128)}, u32[]{:S(2)}) copy-start(f32[128,64]{0,1:T(8,128)} %param.40) | copy-start | bytes 98308
  46.3 184.6 %all-gather.2.cloned.1.call-start = ((), (), s32[]{:S(2)}) async-start(), calls=%async_computation | async-start | bytes 3620864 | tf_op jit(solution)/shard_map/all_gather | solution.py:33
  181.7 0.7 copy-start.4
Sparse Core Ops, SparseCore 0:
  46.4 124.9 all-reduce.3
  182.5 48.3 all-gather.1
where the time goes:
time: 247 us; the launch traced here: 246 us
  waiting for transfers between devices  172 us (70%)
  local copies, waits for them, and re-layouts  50.1 us (20%)
  between operations  15 us (6%)
  other arithmetic  9.27 us (4%)
    unnamed x3, waiting for transfers between devices  123 us
    all_gather x1, waiting for transfers between devices, rows_first(): filled = lax.all_gather(both, axis, axis=0, tiled=True)  48.5 us
    unnamed x54, local copies, waits for them, and re-layouts  16.9 us
    unnamed x7, other arithmetic  6.97 us
    pad x1, local copies, waits for them, and re-layouts, sum_packed(): jnp.pad(lines, ((0, 0), (0, span * 128 - lines.shape[1]))).reshape(-1, 128)  5.84 us
    another operation x4, local copies, waits for them, and re-layouts, sum_packed(): lines = jnp.concatenate([b.reshape(devices, -1) for b in tiles], axis=1)  5.48 us
    reshape x1, local copies, waits for them, and re-layouts, sum_packed(): jnp.pad(lines, ((0, 0), (0, span * 128 - lines.shape[1]))).reshape(-1, 128)  5.03 us
  transfers between devices with their start and end apart: 2, of which 2 were waited for; matrix products, arithmetic and copies ran while one was open for 0% of the time, Pallas kernels for 0%

commit v1 on v0

v1 whole, which is shorter than its diff:
```python
import jax
import jax.numpy as jnp
from jax import lax
from jax.experimental import pallas as pl
from jax.experimental.pallas import tpu as pltpu
from jax.sharding import PartitionSpec as P

learn_rate = 0.1
hold_rate = 0.7

SIDE = 4
LANES = 128
ROWS = 64
NAMES = ("up", "down", "query", "key", "value", "mixed")
ROW_CUT = ("up", "query", "key", "value")

PIECES = (
    (("up", 0), ("up", 1), ("up", 2), ("up", 3), ("query", 0), ("key", 0)),
    (("value", 0), ("mixed", 0), ("down", 0), ("down", 1), ("down", 2), ("down", 3)),
)
SEGMENTS = (1, 1, 1, 1, 1, 1)
HALF_ROWS = ROWS * 6
AXES = (("y", "x"), ("x", "y"))
F32, BF16 = jnp.float32, jnp.bfloat16


def low_lanes(shape):
    return lax.broadcasted_iota(jnp.int32, shape, len(shape) - 1) < LANES // 2


def swap_sides(value):
    return pltpu.roll(value, LANES // 2, len(value.shape) - 1)


def interleave(first, second):
    low = low_lanes(first.shape)
    return jnp.where(low, first, swap_sides(second)), jnp.where(low, swap_sides(first), second)


def segment_spans():
    spans, at = [], 0
    for count in SEGMENTS:
        spans.append((at, count))
        at += count
    return spans


def count_remote():
    return 2 * len(SEGMENTS) * 20 + 6


def exchange_kernel(*refs):
    refs = list(refs)

    def take(count):
        got, refs[:] = refs[:count], refs[count:]
        return got

    grad = dict(zip(NAMES, take(6)))
    (grad_norm,) = take(1)
    weight = dict(zip(NAMES, take(6)))
    (weight_norm,) = take(1)
    moment = dict(zip(NAMES, take(6)))
    (moment_norm,) = take(1)
    full = take(2)
    full_down, full_mixed = take(2)
    new_rows, state_rows = take(2), take(2)
    new_down, state_down, new_mixed, state_mixed = take(4)
    copy_norm, new_norm, state_norm = take(3)
    landed = take(2)
    packed, part = take(2), take(2)
    from_1, from_2 = take(2), take(2)
    weight_in = dict(zip(NAMES, take(6)))
    moment_in = dict(zip(NAMES, take(6)))
    weight_packed, moment_packed = take(2), take(2)
    norm_grad_in, norm_weight_in, norm_moment_in, norm_tiles = take(4)
    load_sem, send_sem, recv_sem = take(3)
    assert not refs

    me = lax.axis_index("batch")
    here = {"y": lax.div(me, SIDE), "x": lax.rem(me, SIDE)}
    step = {a: {d: lax.rem(here[a] + d + SIDE, SIDE) for d in (-1, 1, 2)} for a in ("y", "x")}

    def device(axis, d):
        at = dict(here)
        at[axis] = step[axis][d]
        return {"batch": at["y"] * SIDE + at["x"]}

    barrier = pltpu.get_barrier_semaphore()
    for axis in ("y", "x"):
        for d in (-1, 1):
            pl.semaphore_signal(barrier, inc=1, device_id=device(axis, d), device_id_type=pl.DeviceIdType.MESH)

    loads = {}

    def load(key, source, target):
        copy = pltpu.make_async_copy(source, target, load_sem.at[len(loads)])
        copy.start()
        loads[key] = copy

    for k in range(6):
        for half in (0, 1):
            name, part_no = PIECES[half][k]
            if name in ROW_CUT:
                load((half, k), grad[name].at[0, :, pl.ds(part_no * LANES, LANES)], landed[0].at[slot_of(half, k)])
            else:
                load((half, k), grad[name].at[0, pl.ds(part_no * LANES, LANES), :], landed[1].at[slot_of(half, k)])
        if k == 0:
            load("norm_grad", grad_norm, norm_grad_in)
            load("norm_weight", weight_norm, norm_weight_in)
            load("norm_moment", moment_norm, norm_moment_in)
    for name in NAMES:
        load(("weight", name), weight[name], weight_in[name])
        load(("moment", name), moment[name], moment_in[name])

    def pack_piece(half, k):
        name, part_no = PIECES[half][k]
        loads[half, k].wait()
        rows = pl.ds(k * ROWS, ROWS)
        slot = slot_of(half, k)

        def put(b, value):
            y, x = divmod(b, SIDE)
            at = (y, x) if AXES[half][0] == "y" else (x, y)
            packed[half][at[0], at[1], rows, :] = value.astype(BF16)

        if name in ROW_CUT:
            for b in range(SIDE * SIDE):
                put(b, landed[0][slot, b * ROWS : (b + 1) * ROWS, :])
        else:
            for m in range(SIDE * SIDE // 2):
                lanes = slice(m * LANES, (m + 1) * LANES)
                pair = interleave(landed[1][slot, :ROWS, lanes], landed[1][slot, ROWS:, lanes])
                put(2 * m, pair[0])
                put(2 * m + 1, pair[1])

    def pack_own():
        for half in (0, 1):
            for k, (name, part_no) in enumerate(PIECES[half]):
                rows = pl.ds(k * ROWS, ROWS)
                if part_no == 0:
                    loads["weight", name].wait()
                    loads["moment", name].wait()
                for source, target in ((weight_in[name], weight_packed[half]), (moment_in[name], moment_packed[half])):
                    if name in ROW_CUT:
                        target[rows, :] = source[:, part_no * LANES : (part_no + 1) * LANES]
                    else:
                        turned = source[:, part_no * LANES : (part_no + 1) * LANES].T
                        target[rows, :] = jnp.concatenate([turned[:ROWS, :], turned[ROWS:, :]], axis=1)

    sent = {}

    def send(key, source, target, axis, d):
        n = len(sent)
        copy = pltpu.make_async_remote_copy(
            src_ref=source,
            dst_ref=target,
            send_sem=send_sem.at[n],
            recv_sem=recv_sem.at[n],
            device_id=device(axis, d),
            device_id_type=pl.DeviceIdType.MESH,
        )
        copy.start()
        sent[key] = copy

    def arrived(key):
        sent[key].wait_recv()

    def spans(s):
        at, count = segment_spans()[s]
        rows, side = at * ROWS, count * ROWS // 2
        return (pl.ds(rows, side), pl.ds(rows + side, side), pl.ds(rows // 2, side), pl.ds(rows, 2 * side))

    def reduce_send(half, level, s):
        axis = AXES[half][level]
        low, high, place, _ = spans(s)
        data = (packed, part)[level][half]
        land = (from_1, from_2)[level][half]

        def src(d, rows):
            return data.at[step[axis][d], :, rows, :] if level == 0 else data.at[step[axis][d], rows, :]

        def dst(kind, d):
            return land.at[kind, 0 if d == 1 else 1, :, place, :] if level == 0 else land.at[kind, 0 if d == 1 else 1, place, :]

        send((half, level, s, 0, 1), src(2, low), dst(0, 1), axis, 1)
        send((half, level, s, 0, -1), src(2, high), dst(0, -1), axis, -1)
        send((half, level, s, 1, 1), src(1, high), dst(1, 1), axis, 1)
        send((half, level, s, 1, -1), src(-1, low), dst(1, -1), axis, -1)

    def reduce_forward(half, level, s):
        axis = AXES[half][level]
        low, high, place, _ = spans(s)
        data = (packed, part)[level][half]
        land = (from_1, from_2)[level][half]
        for d, rows in ((1, low), (-1, high)):
            arrived((half, level, s, 0, d))
            side = 0 if d == 1 else 1
            to = step[axis][d]
            if level == 0:
                total = data[to, :, rows, :].astype(F32) + land[0, side, :, place, :].astype(F32)
                data[to, :, rows, :] = total.astype(BF16)
                send((half, level, s, 2, d), data.at[to, :, rows, :], land.at[2, side, :, place, :], axis, d)
            else:
                total = data[to, rows, :].astype(F32) + land[0, side, place, :].astype(F32)
                data[to, rows, :] = total.astype(BF16)
                send((half, level, s, 2, d), data.at[to, rows, :], land.at[2, side, place, :], axis, d)

    def reduce_totals(half, level, s):
        axis = AXES[half][level]
        low, high, place, _ = spans(s)
        data = (packed, part)[level][half]
        land = (from_1, from_2)[level][half]
        arrived((half, level, s, 1, 1))
        arrived((half, level, s, 1, -1))
        arrived((half, level, s, 2, 1))
        arrived((half, level, s, 2, -1))
        mine = here[axis]
        for rows, (first, second) in ((low, ((2, 0), (1, 1))), (high, ((1, 0), (2, 1)))):
            if level == 0:
                total = data[mine, :, rows, :].astype(F32)
                total += land[first[0], first[1], :, place, :].astype(F32)
                total += land[second[0], second[1], :, place, :].astype(F32)
            else:
                total = data[mine, rows, :].astype(F32)
                total += land[first[0], first[1], place, :].astype(F32)
                total += land[second[0], second[1], place, :].astype(F32)
            yield rows, total

    def first_totals(half, s):
        for rows, total in reduce_totals(half, 0, s):
            part[half][:, rows, :] = total.astype(BF16)

    mean_rate = float(SIDE * SIDE) ** -0.5

    def update(half, s):
        first, second = AXES[half]
        for rows, total in reduce_totals(half, 1, s):
            state = hold_rate * moment_packed[half][rows, :] + total * mean_rate
            new = weight_packed[half][rows, :] - learn_rate * state
            state_rows[half][rows, :] = state
            new_rows[half][rows, :] = new
            full[half][here[first], here[second], rows, :] = new.astype(BF16)
        at, count = segment_spans()[s]
        for k in range(at, at + count):
            name, part_no = PIECES[half][k]
            if name in ROW_CUT:
                continue
            rows = pl.ds(k * ROWS, ROWS)
            targets = (new_down, state_down) if name == "down" else (new_mixed, state_mixed)
            for source, target in zip((new_rows[half], state_rows[half]), targets):
                turned = source[rows, :].T
                target[:, part_no * LANES : (part_no + 1) * LANES] = jnp.concatenate([turned[:ROWS, :], turned[ROWS:, :]], axis=1)

    def gather_part(half, level, d, rows):
        first, second = AXES[half]
        if level == 1:
            at = here[second] if d == 0 else step[second][d]
            return full[half].at[here[first], at, rows, :]
        at = here[first] if d == 0 else step[first][d]
        return full[half].at[at, :, rows, :]

    def gather_send(half, level, s):
        whole = spans(s)[3]
        axis = AXES[half][level]
        block = gather_part(half, level, 0, whole)
        for d in (1, -1):
            send((half, level, s, 3, d), block, block, axis, d)

    def gather_forward(half, level, s):
        low, high, _, _ = spans(s)
        axis = AXES[half][level]
        for d, rows in ((1, low), (-1, high)):
            arrived((half, level, s, 3, d))
            block = gather_part(half, level, -d, rows)
            send((half, level, s, 4, d), block, block, axis, d)

    def gather_end(half, level, s):
        arrived((half, level, s, 4, 1))
        arrived((half, level, s, 4, -1))

    def unpack(half, s):
        at, count = segment_spans()[s]
        for k in range(at, at + count):
            name, part_no = PIECES[half][k]
            if name in ROW_CUT:
                continue
            target = full_down if name == "down" else full_mixed
            rows = pl.ds(k * ROWS, ROWS)
            for m in range(SIDE * SIDE // 2):
                pair = []
                for b in (2 * m, 2 * m + 1):
                    y, x = divmod(b, SIDE)
                    at_ = (y, x) if AXES[half][0] == "y" else (x, y)
                    pair.append(full[half][at_[0], at_[1], rows, :].astype(F32))
                top, bottom = interleave(*pair)
                lanes = slice(m * LANES, (m + 1) * LANES)
                target[part_no * LANES : part_no * LANES + ROWS, lanes] = top.astype(BF16)
                target[part_no * LANES + ROWS : (part_no + 1) * LANES, lanes] = bottom.astype(BF16)

    def norm_start():
        for key in ("norm_grad", "norm_weight", "norm_moment"):
            loads[key].wait()
        for k in range(8):
            norm_tiles[0, k : k + 1, :] = norm_grad_in[0:1, k * LANES : (k + 1) * LANES]
        base = norm_weight_in[...] - learn_rate * (hold_rate * norm_moment_in[...])
        base = jnp.broadcast_to(jnp.concatenate([base, base], axis=1), (8, LANES))
        row = lax.broadcasted_iota(jnp.int32, (8, LANES), 0)
        owner = 2 * row + jnp.where(low_lanes((8, LANES)), 0, 1)
        norm_tiles[0, 8:16, :] = jnp.where(owner == me, base, 0.0)
        norm_send("y", 0)

    def norm_send(axis, at):
        for d in (1, -1):
            send(("norm", axis, d), norm_tiles.at[at], norm_tiles.at[at + (1 if d == 1 else 2)], axis, d)

    def norm_forward(axis, at):
        arrived(("norm", axis, 1))
        send(("norm", axis, 2), norm_tiles.at[at + 1], norm_tiles.at[at + 3], axis, 1)

    def norm_total(axis, at):
        arrived(("norm", axis, -1))
        arrived(("norm", axis, 2))
        return (norm_tiles[at] + norm_tiles[at + 1]) + (norm_tiles[at + 2] + norm_tiles[at + 3])

    def norm_middle():
        norm_tiles[4] = norm_total("y", 0)
        norm_send("x", 4)

    def norm_end():
        total = norm_total("x", 4)
        mean = total[0:8, :] * mean_rate
        norm_tiles[8, 0:8, :] = mean
        new = (total[8:16, :] - learn_rate * mean).astype(BF16)
        for k in range(8):
            copy_norm[0:1, k * LANES : (k + 1) * LANES] = new[k : k + 1, :]
        own = norm_tiles[8, pl.ds(lax.div(me, 2), 1), :]
        own = jnp.where(lax.rem(me, 2) == 1, swap_sides(own), own)[:, : LANES // 2]
        state = hold_rate * norm_moment_in[...] + own
        state_norm[...] = state
        new_norm[...] = norm_weight_in[...] - learn_rate * state

    def begin(half, s):
        at, count = segment_spans()[s]
        for k in range(at, at + count):
            pack_piece(half, k)
        if half == 0 and s == 0:
            pl.semaphore_wait(barrier, 4)
        reduce_send(half, 0, s)

    def second_send(half, s):
        first_totals(half, s)
        reduce_send(half, 1, s)

    def share(half, s):
        update(half, s)
        gather_send(half, 1, s)

    def second_share(half, s):
        gather_end(half, 1, s)
        gather_send(half, 0, s)

    def finish(half, s):
        gather_end(half, 0, s)
        unpack(half, s)

    stages = (
        begin,
        lambda half, s: reduce_forward(half, 0, s),
        second_send,
        lambda half, s: reduce_forward(half, 1, s),
        share,
        lambda half, s: gather_forward(half, 1, s),
        second_share,
        lambda half, s: gather_forward(half, 0, s),
        finish,
    )
    count = len(SEGMENTS)
    for t in range(count + len(stages) - 1):
        for n, stage in enumerate(stages):
            if 0 <= t - n < count:
                for half in (0, 1):
                    stage(half, t - n)
        if t == 0:
            norm_start()
            pack_own()
        if t == 2:
            norm_forward("y", 0)
        if t == 3:
            norm_middle()
        if t == 5:
            norm_forward("x", 4)
        if t == 7:
            norm_end()
    for copy in sent.values():
        copy.wait_send()


def slot_of(half, k):
    order = [p for h in (0, 1) for p in PIECES[h]]
    this = PIECES[half][k]
    kind = this[0] in ROW_CUT
    return [p for p in order if (p[0] in ROW_CUT) == kind].index(this)


def place_kernel(*refs):
    refs = list(refs)

    def take(count):
        got, refs[:] = refs[:count], refs[count:]
        return got

    full = take(2)
    full_down, full_mixed = take(2)
    new_rows, state_rows = take(2), take(2)
    new_down_in, state_down_in, new_mixed_in, state_mixed_in = take(4)
    norms_in = take(3)
    copy_out = dict(zip(ROW_CUT, take(4)))
    copy_down, copy_mixed = take(2)
    new_out = dict(zip(ROW_CUT, take(4)))
    new_down, new_mixed = take(2)
    state_out = dict(zip(ROW_CUT, take(4)))
    state_down, state_mixed = take(2)
    norms_out = take(3)
    (sem,) = take(1)
    assert not refs
    copies = []

    def put(source, target):
        copies.append(pltpu.make_async_copy(source, target, sem.at[len(copies)]))
        copies[-1].start()

    for half in (0, 1):
        for k, (name, part_no) in enumerate(PIECES[half]):
            if name not in ROW_CUT:
                continue
            rows, lanes = pl.ds(k * ROWS, ROWS), pl.ds(part_no * LANES, LANES)
            if AXES[half][0] == "y":
                put(full[half].at[:, :, rows, :], copy_out[name].at[:, :, :, lanes])
            else:
                for n in range(SIDE):
                    put(full[half].at[n, :, rows, :], copy_out[name].at[:, n, :, lanes])
            put(new_rows[half].at[rows, :], new_out[name].at[:, lanes])
            put(state_rows[half].at[rows, :], state_out[name].at[:, lanes])
    put(full_down, copy_down)
    put(full_mixed, copy_mixed)
    put(new_down_in, new_down)
    put(state_down_in, state_down)
    put(new_mixed_in, new_mixed)
    put(state_mixed_in, state_mixed)
    for source, target in zip(norms_in, norms_out):
        put(source, target)
    for copy in copies:
        copy.wait()


PLACE_COPIES = 2 + 4 + 6 * 2 + 4 + 4 + 2 * 7 + 3


def in_hbm(arrays):
    return [pltpu.with_memory_space_constraint(a, pltpu.HBM) for a in arrays]


def body(*arrays):
    arrays = [a.T if a.ndim == 2 and a.shape[1] == ROWS else a for a in arrays]
    grads, weights, moments = arrays[:7], arrays[7:14], arrays[14:]
    shapes = [w.shape for w in weights[:6]]
    half = jax.ShapeDtypeStruct((SIDE, SIDE, HALF_ROWS, LANES), BF16)
    rows = jax.ShapeDtypeStruct((HALF_ROWS, LANES), F32)
    down, mixed = jax.ShapeDtypeStruct(shapes[1], F32), jax.ShapeDtypeStruct(shapes[5], F32)
    held = (
        half,
        half,
        jax.ShapeDtypeStruct(grads[1].shape[1:], BF16),
        jax.ShapeDtypeStruct(grads[5].shape[1:], BF16),
        rows,
        rows,
        rows,
        rows,
        down,
        down,
        mixed,
        mixed,
        jax.ShapeDtypeStruct((1, 8 * LANES), BF16),
        jax.ShapeDtypeStruct((1, LANES // 2), F32),
        jax.ShapeDtypeStruct((1, LANES // 2), F32),
    )
    dma = pltpu.SemaphoreType.DMA
    remote = count_remote()
    vmem = pl.BlockSpec(memory_space=pltpu.VMEM)
    anywhere = pl.BlockSpec(memory_space=pltpu.HBM)
    half_scratch = pltpu.VMEM((SIDE, SIDE, HALF_ROWS, LANES), BF16)
    part_scratch = pltpu.VMEM((SIDE, HALF_ROWS, LANES), BF16)
    from_1 = pltpu.VMEM((3, 2, SIDE, HALF_ROWS // 2, LANES), BF16)
    from_2 = pltpu.VMEM((3, 2, HALF_ROWS // 2, LANES), BF16)
    own = [pltpu.VMEM(s, F32) for s in shapes]
    own_packed = pltpu.VMEM((HALF_ROWS, LANES), F32)
    small = pltpu.VMEM((1, LANES // 2), F32)
    results = pl.pallas_call(
        exchange_kernel,
        out_shape=held,
        in_specs=[anywhere] * 21,
        out_specs=[vmem] * len(held),
        scratch_shapes=[
            pltpu.VMEM((7, SIDE * SIDE * ROWS, LANES), F32),
            pltpu.VMEM((5, LANES, SIDE * SIDE * ROWS), F32),
            half_scratch,
            half_scratch,
            part_scratch,
            part_scratch,
            from_1,
            from_1,
            from_2,
            from_2,
            *own,
            *own,
            own_packed,
            own_packed,
            own_packed,
            own_packed,
            pltpu.VMEM((1, 8 * LANES), F32),
            small,
            small,
            pltpu.VMEM((9, 16, LANES), F32),
            dma((27,)),
            dma((remote,)),
            dma((remote,)),
        ],
        compiler_params=pltpu.CompilerParams(
            collective_id=0, has_side_effects=True, vmem_limit_bytes=32 * 1024 * 1024
        ),
        name="exchange",
    )(
        *in_hbm(grads),
        *in_hbm(weights[:6]),
        *in_hbm([weights[6].reshape(1, -1)]),
        *in_hbm(moments[:6]),
        *in_hbm([moments[6].reshape(1, -1)]),
    )
    row_shapes = [shapes[NAMES.index(n)] for n in ROW_CUT]
    tall = [jax.ShapeDtypeStruct((SIDE, SIDE, *s), BF16) for s in row_shapes]
    own_rows = [jax.ShapeDtypeStruct(s, F32) for s in row_shapes]
    placed = pl.pallas_call(
        place_kernel,
        out_shape=(*tall, held[2], held[3], *own_rows, down, mixed, *own_rows, down, mixed, *held[12:]),
        in_specs=[vmem] * 15,
        out_specs=[anywhere] * 21,
        scratch_shapes=[dma((PLACE_COPIES,))],
        compiler_params=pltpu.CompilerParams(vmem_limit_bytes=16 * 1024 * 1024),
        name="place",
    )(*results)
    outs = []
    for k, last in zip((0, 6, 12), placed[18:]):
        up, query, key, value, down_, mixed_ = placed[k : k + 6]
        group = [up, down_, query, key, value, mixed_]
        if k == 0:
            group = [g.reshape(-1, g.shape[-1]) for g in group]
        else:
            group[1], group[5] = group[1].T, group[5].T
        outs += [*group, last.reshape(-1)]
    return tuple(outs)


def solution(mesh):
    cut_rows, cut_columns = P("batch", "cols"), P("cols", "batch")
    own = (cut_rows, cut_columns, cut_rows, cut_rows, cut_rows, cut_columns, P("batch"))
    grad_rows, grad_columns = P("batch", None, "cols"), P("batch", "cols", None)
    grads = (grad_rows, grad_columns, grad_rows, grad_rows, grad_rows, grad_columns, P("batch", None))
    whole_rows, whole_columns = P(None, "cols"), P("cols", None)
    copies = (whole_rows, whole_columns, whole_rows, whole_rows, whole_rows, whole_columns, P())
    return jax.shard_map(
        body, mesh=mesh, in_specs=(*grads, *own, *own), out_specs=(*copies, *own, *own), check_vma=False
    )
```

time: 247 us -> 56.4 us (0.23)
  waiting for transfers between devices: 172 us -> 0 us
  Pallas kernels: 0 us -> 55 us
  local copies, waits for them, and re-layouts: 50.1 us -> 0 us
  between operations: 15 us -> 0.68 us
  other arithmetic: 9.27 us -> 0.6 us
    unnamed x3 -> x0, waiting for transfers between devices: 123 us -> none
    pallas_call x0 -> x2, Pallas kernels: none -> 55 us  [the longest x1 52.7 us: body(): pl.pallas_call(exchange_kernel, out_shape=held, in_specs=[anywhere] * 21,...]
    all_gather x1 -> x0, waiting for transfers between devices: 48.5 us -> none  [rows_first(): filled = lax.all_gather(both, axis, axis=0, tiled=True)]
    unnamed x54 -> x0, local copies, waits for them, and re-layouts: 16.9 us -> none
    reshape x5 -> x0, local copies, waits for them, and re-layouts: 10.3 us -> none  [the longest x1 5.03 us: sum_packed(): jnp.pad(lines, ((0, 0), (0, span * 128 - lines.shape[1]))).reshape(-1, 128)]
    transpose x4 -> x0, local copies, waits for them, and re-layouts: 8.85 us -> none  [the longest x2 4.76 us: rows_first(): jnp.moveaxis(b.reshape(-1, *t.shape[1:]), 0, dim)]
    unnamed x7 -> x0, other arithmetic: 6.97 us -> none
    pad x1 -> x0, local copies, waits for them, and re-layouts: 5.84 us -> none  [sum_packed(): jnp.pad(lines, ((0, 0), (0, span * 128 - lines.shape[1]))).reshape(-1, 128)]
  transfers between devices with their start and end apart: 2 -> 0, of which waited for: 2 -> 0; matrix products, arithmetic and copies ran while one was open for 0% -> 0% of each run, Pallas kernels for 0% -> 0%
where the time goes in v1:
time: 56.4 us; the launch traced here: 56.3 us
  Pallas kernels  55 us (98%)
  between operations  0.68 us (1%)
  other arithmetic  0.6 us (1%)
    pallas_call x1, Pallas kernels, body(): pl.pallas_call(exchange_kernel, out_shape=held, in_specs=[anywhere] * 21,...  52.7 us
    pallas_call x1, Pallas kernels, body(): pl.pallas_call(place_kernel, out_shape=(*tall, held[2], held[3], *own_row...  2.34 us

profile of v1, /device:TPU:0, one launch (start us, length us, event | category | flops | bytes accessed | tf_op | source)
XLA Modules:
  0.0 56.3 jit_solution(6240054515534109409)
XLA Ops:
  0.7 52.7 %exchange.1 = (bf16[4,4,384,128]{3,2,1,0:T(8,128)(2,1)S(1)}, bf16[4,4,384,128]{3,2,1,0:T(8,128)(2,1)S(1)}, bf16[512,1024]{1,0:T(8,128)(2,1)S(1)}, bf16[128,1024]...) custom-call(f32[1,1024,512]{2,1,0:T(8,128)} %refs_0_.1, ...), custom_call_target="tpu_custom_call" | custom-call | tf_op jit(solution)/shard_map/exchange/pallas_call | solution.py:499
  53.3 2.3 %place.1 = (bf16[4,4,64,512]{3,2,1,0:T(8,128)(2,1)}, bf16[4,4,64,128]{3,2,1,0:T(8,128)(2,1)}, bf16[4,4,64,128]{3,2,1,0:T(8,128)(2,1)}, bf16[4,4,64,128]{3,2,1,0:...) custom-call(bf16[4,4,384,128]{3,2,1,0:T(8,128)(2,1)S(1)} %get-tuple-, ...), custom_call_target="tpu_custom_call" | custom-call | tf_op jit(solution)/shard_map/place/pallas_call | solution.py:543
  55.7 0.6 %reduce = bf16[1024]{0:T(1024)(128)(2,1)} reduce(bf16[1,1024]{1,0:T(2,128)(2,1)S(1)} %get-tuple-element.78, bf16[]{:T(256)} %constant.7), dimensions={0}, to_apply=%get-tuple-element.78.reduce_sub_computation | reduce | bytes 4098 | tf_op jit(solution)/shard_map/place/pallas_call | solution.py:543

commit v2 on v1

--- a/solution.py
+++ b/solution.py
@@ -18,9 +18,10 @@
     (("up", 0), ("up", 1), ("up", 2), ("up", 3), ("query", 0), ("key", 0)),
     (("value", 0), ("mixed", 0), ("down", 0), ("down", 1), ("down", 2), ("down", 3)),
 )
-SEGMENTS = (1, 1, 1, 1, 1, 1)
+SEGMENTS = (2, 3, 1)
 HALF_ROWS = ROWS * 6
 AXES = (("y", "x"), ("x", "y"))
+AWAY = (1, -1, 2)
 F32, BF16 = jnp.float32, jnp.bfloat16
 
 
@@ -46,7 +47,7 @@
 
 
 def count_remote():
-    return 2 * len(SEGMENTS) * 20 + 6
+    return 2 * len(SEGMENTS) * 16 + 6
 
 
 def exchange_kernel(*refs):
@@ -79,18 +80,13 @@
 
     me = lax.axis_index("batch")
     here = {"y": lax.div(me, SIDE), "x": lax.rem(me, SIDE)}
-    step = {a: {d: lax.rem(here[a] + d + SIDE, SIDE) for d in (-1, 1, 2)} for a in ("y", "x")}
+    step = {a: {d: lax.rem(here[a] + d + SIDE, SIDE) for d in AWAY} for a in ("y", "x")}
 
     def device(axis, d):
         at = dict(here)
         at[axis] = step[axis][d]
         return {"batch": at["y"] * SIDE + at["x"]}
 
-    barrier = pltpu.get_barrier_semaphore()
-    for axis in ("y", "x"):
-        for d in (-1, 1):
-            pl.semaphore_signal(barrier, inc=1, device_id=device(axis, d), device_id_type=pl.DeviceIdType.MESH)
-
     loads = {}
 
     def load(key, source, target):
@@ -98,20 +94,30 @@
         copy.start()
         loads[key] = copy
 
-    for k in range(6):
-        for half in (0, 1):
+    def load_segment(half, s):
+        at, count = segment_spans()[s]
+        for k in range(at, at + count):
             name, part_no = PIECES[half][k]
+            lanes = pl.ds(part_no * LANES, LANES)
             if name in ROW_CUT:
-                load((half, k), grad[name].at[0, :, pl.ds(part_no * LANES, LANES)], landed[0].at[slot_of(half, k)])
+                load((half, k), grad[name].at[0, :, lanes], landed[0].at[slot_of(half, k)])
             else:
-                load((half, k), grad[name].at[0, pl.ds(part_no * LANES, LANES), :], landed[1].at[slot_of(half, k)])
-        if k == 0:
-            load("norm_grad", grad_norm, norm_grad_in)
-            load("norm_weight", weight_norm, norm_weight_in)
-            load("norm_moment", moment_norm, norm_moment_in)
-    for name in NAMES:
-        load(("weight", name), weight[name], weight_in[name])
-        load(("moment", name), moment[name], moment_in[name])
+                load((half, k), grad[name].at[0, lanes, :], landed[1].at[slot_of(half, k)])
+
+    def load_own():
+        load("norm_grad", grad_norm, norm_grad_in)
+        load("norm_weight", weight_norm, norm_weight_in)
+        load("norm_moment", moment_norm, norm_moment_in)
+        for name in NAMES:
+            load(("weight", name), weight[name], weight_in[name])
+            load(("moment", name), moment[name], moment_in[name])
+
+    for half in (0, 1):
+        load_segment(half, 0)
+    barrier = pltpu.get_barrier_semaphore()
+    for axis in ("y", "x"):
+        for d in AWAY:
+            pl.semaphore_signal(barrier, inc=1, device_id=device(axis, d), device_id_type=pl.DeviceIdType.MESH)
 
     def pack_piece(half, k):
         name, part_no = PIECES[half][k]
@@ -171,76 +177,62 @@
         rows, side = at * ROWS, count * ROWS // 2
         return (pl.ds(rows, side), pl.ds(rows + side, side), pl.ds(rows // 2, side), pl.ds(rows, 2 * side))
 
-    def reduce_send(half, level, s):
-        axis = AXES[half][level]
+    def first_send(half, s):
+        axis = AXES[half][0]
         low, high, place, _ = spans(s)
-        data = (packed, part)[level][half]
-        land = (from_1, from_2)[level][half]
-
-        def src(d, rows):
-            return data.at[step[axis][d], :, rows, :] if level == 0 else data.at[step[axis][d], rows, :]
-
-        def dst(kind, d):
-            return land.at[kind, 0 if d == 1 else 1, :, place, :] if level == 0 else land.at[kind, 0 if d == 1 else 1, place, :]
-
-        send((half, level, s, 0, 1), src(2, low), dst(0, 1), axis, 1)
-        send((half, level, s, 0, -1), src(2, high), dst(0, -1), axis, -1)
-        send((half, level, s, 1, 1), src(1, high), dst(1, 1), axis, 1)
-        send((half, level, s, 1, -1), src(-1, low), dst(1, -1), axis, -1)
-
-    def reduce_forward(half, level, s):
-        axis = AXES[half][level]
+        data, land = packed[half], from_1[half]
+        send((half, s, 0, 1), data.at[step[axis][2], :, low, :], land.at[0, 0, :, place, :], axis, 1)
+        send((half, s, 0, -1), data.at[step[axis][2], :, high, :], land.at[0, 1, :, place, :], axis, -1)
+        send((half, s, 1, 1), data.at[step[axis][1], :, high, :], land.at[1, 0, :, place, :], axis, 1)
+        send((half, s, 1, -1), data.at[step[axis][-1], :, low, :], land.at[1, 1, :, place, :], axis, -1)
+
+    def first_forward(half, s):
+        axis = AXES[half][0]
         low, high, place, _ = spans(s)
-        data = (packed, part)[level][half]
-        land = (from_1, from_2)[level][half]
-        for d, rows in ((1, low), (-1, high)):
-            arrived((half, level, s, 0, d))
-            side = 0 if d == 1 else 1
+        data, land = packed[half], from_1[half]
+        for side, d, rows in ((0, 1, low), (1, -1, high)):
+            arrived((half, s, 0, d))
             to = step[axis][d]
-            if level == 0:
-                total = data[to, :, rows, :].astype(F32) + land[0, side, :, place, :].astype(F32)
-                data[to, :, rows, :] = total.astype(BF16)
-                send((half, level, s, 2, d), data.at[to, :, rows, :], land.at[2, side, :, place, :], axis, d)
-            else:
-                total = data[to, rows, :].astype(F32) + land[0, side, place, :].astype(F32)
-                data[to, rows, :] = total.astype(BF16)
-                send((half, level, s, 2, d), data.at[to, rows, :], land.at[2, side, place, :], axis, d)
-
-    def reduce_totals(half, level, s):
-        axis = AXES[half][level]
-        low, high, place, _ = spans(s)
-        data = (packed, part)[level][half]
-        land = (from_1, from_2)[level][half]
-        arrived((half, level, s, 1, 1))
-        arrived((half, level, s, 1, -1))
-        arrived((half, level, s, 2, 1))
-        arrived((half, level, s, 2, -1))
-        mine = here[axis]
-        for rows, (first, second) in ((low, ((2, 0), (1, 1))), (high, ((1, 0), (2, 1)))):
-            if level == 0:
-                total = data[mine, :, rows, :].astype(F32)
-                total += land[first[0], first[1], :, place, :].astype(F32)
-                total += land[second[0], second[1], :, place, :].astype(F32)
-            else:
-                total = data[mine, rows, :].astype(F32)
-                total += land[first[0], first[1], place, :].astype(F32)
-                total += land[second[0], second[1], place, :].astype(F32)
-            yield rows, total
-
-    def first_totals(half, s):
-        for rows, total in reduce_totals(half, 0, s):
+            total = data[to, :, rows, :].astype(F32) + land[0, side, :, place, :].astype(F32)
+            data[to, :, rows, :] = total.astype(BF16)
+            send((half, s, 2, d), data.at[to, :, rows, :], land.at[2, side, :, place, :], axis, d)
+
+    def second_send(half, s):
+        low, high, place, whole = spans(s)
+        data, land = packed[half], from_1[half]
+        for kind in (1, 2):
+            for d in (1, -1):
+                arrived((half, s, kind, d))
+        mine = here[AXES[half][0]]
+        for rows, first, second in ((low, 2, 1), (high, 1, 2)):
+            total = data[mine, :, rows, :].astype(F32)
+            total += land[first, 0, :, place, :].astype(F32)
+            total += land[second, 1, :, place, :].astype(F32)
             part[half][:, rows, :] = total.astype(BF16)
+        axis = AXES[half][1]
+        for n, d in ((2, 2), (0, 1), (1, -1)):
+            send((half, s, 3, d), part[half].at[step[axis][d], whole, :], from_2[half].at[n, whole, :], axis, d)
 
     mean_rate = float(SIDE * SIDE) ** -0.5
 
     def update(half, s):
         first, second = AXES[half]
-        for rows, total in reduce_totals(half, 1, s):
-            state = hold_rate * moment_packed[half][rows, :] + total * mean_rate
-            new = weight_packed[half][rows, :] - learn_rate * state
-            state_rows[half][rows, :] = state
-            new_rows[half][rows, :] = new
-            full[half][here[first], here[second], rows, :] = new.astype(BF16)
+        whole = spans(s)[3]
+        for d in AWAY:
+            arrived((half, s, 3, d))
+        total = part[half][here[second], whole, :].astype(F32)
+        for n in range(3):
+            total += from_2[half][n, whole, :].astype(F32)
+        state = hold_rate * moment_packed[half][whole, :] + total * mean_rate
+        new = weight_packed[half][whole, :] - learn_rate * state
+        state_rows[half][whole, :] = state
+        new_rows[half][whole, :] = new
+        full[half][here[first], here[second], whole, :] = new.astype(BF16)
+        own = full[half].at[here[first], here[second], whole, :]
+        for d in (2, 1, -1):
+            send((half, s, 4, d), own, own, second, d)
+
+    def turn_own(half, s):
         at, count = segment_spans()[s]
         for k in range(at, at + count):
             name, part_no = PIECES[half][k]
@@ -252,32 +244,22 @@
                 turned = source[rows, :].T
                 target[:, part_no * LANES : (part_no + 1) * LANES] = jnp.concatenate([turned[:ROWS, :], turned[ROWS:, :]], axis=1)
 
-    def gather_part(half, level, d, rows):
-        first, second = AXES[half]
-        if level == 1:
-            at = here[second] if d == 0 else step[second][d]
-            return full[half].at[here[first], at, rows, :]
-        at = here[first] if d == 0 else step[first][d]
-        return full[half].at[at, :, rows, :]
-
-    def gather_send(half, level, s):
-        whole = spans(s)[3]
-        axis = AXES[half][level]
-        block = gather_part(half, level, 0, whole)
+    def share(half, s):
+        for d in AWAY:
+            arrived((half, s, 4, d))
+        first = AXES[half][0]
+        block = full[half].at[here[first], :, spans(s)[3], :]
         for d in (1, -1):
-            send((half, level, s, 3, d), block, block, axis, d)
-
-    def gather_forward(half, level, s):
+            send((half, s, 5, d), block, block, first, d)
+        turn_own(half, s)
+
+    def share_forward(half, s):
+        first = AXES[half][0]
         low, high, _, _ = spans(s)
-        axis = AXES[half][level]
         for d, rows in ((1, low), (-1, high)):
-            arrived((half, level, s, 3, d))
-            block = gather_part(half, level, -d, rows)
-            send((half, level, s, 4, d), block, block, axis, d)
-
-    def gather_end(half, level, s):
-        arrived((half, level, s, 4, 1))
-        arrived((half, level, s, 4, -1))
+            arrived((half, s, 5, d))
+            block = full[half].at[step[first][-d], :, rows, :]
+            send((half, s, 6, d), block, block, first, d)
 
     def unpack(half, s):
         at, count = segment_spans()[s]
@@ -311,16 +293,12 @@
         norm_send("y", 0)
 
     def norm_send(axis, at):
-        for d in (1, -1):
-            send(("norm", axis, d), norm_tiles.at[at], norm_tiles.at[at + (1 if d == 1 else 2)], axis, d)
-
-    def norm_forward(axis, at):
-        arrived(("norm", axis, 1))
-        send(("norm", axis, 2), norm_tiles.at[at + 1], norm_tiles.at[at + 3], axis, 1)
+        for n, d in enumerate(AWAY):
+            send(("norm", axis, d), norm_tiles.at[at], norm_tiles.at[at + 1 + n], axis, d)
 
     def norm_total(axis, at):
-        arrived(("norm", axis, -1))
-        arrived(("norm", axis, 2))
+        for d in AWAY:
+            arrived(("norm", axis, d))
         return (norm_tiles[at] + norm_tiles[at + 1]) + (norm_tiles[at + 2] + norm_tiles[at + 3])
 
     def norm_middle():
@@ -333,7 +311,7 @@
         norm_tiles[8, 0:8, :] = mean
         new = (total[8:16, :] - learn_rate * mean).astype(BF16)
         for k in range(8):
-            copy_norm[0:1, k * LANES : (k + 1) * LANES] = new[k : k + 1, :]
+            copy_norm[k * LANES : (k + 1) * LANES] = new[k, :]
         own = norm_tiles[8, pl.ds(lax.div(me, 2), 1), :]
         own = jnp.where(lax.rem(me, 2) == 1, swap_sides(own), own)[:, : LANES // 2]
         state = hold_rate * norm_moment_in[...] + own
@@ -345,53 +323,26 @@
         for k in range(at, at + count):
             pack_piece(half, k)
         if half == 0 and s == 0:
-            pl.semaphore_wait(barrier, 4)
-        reduce_send(half, 0, s)
-
-    def second_send(half, s):
-        first_totals(half, s)
-        reduce_send(half, 1, s)
-
-    def share(half, s):
-        update(half, s)
-        gather_send(half, 1, s)
-
-    def second_share(half, s):
-        gather_end(half, 1, s)
-        gather_send(half, 0, s)
+            pl.semaphore_wait(barrier, 2 * len(AWAY))
+        first_send(half, s)
+        if s + 1 < len(SEGMENTS):
+            load_segment(half, s + 1)
+        elif half == 1:
+            load_own()
 
     def finish(half, s):
-        gather_end(half, 0, s)
+        for d in (1, -1):
+            arrived((half, s, 6, d))
         unpack(half, s)
 
-    stages = (
-        begin,
-        lambda half, s: reduce_forward(half, 0, s),
-        second_send,
-        lambda half, s: reduce_forward(half, 1, s),
-        share,
-        lambda half, s: gather_forward(half, 1, s),
-        second_share,
-        lambda half, s: gather_forward(half, 0, s),
-        finish,
-    )
-    count = len(SEGMENTS)
-    for t in range(count + len(stages) - 1):
-        for n, stage in enumerate(stages):
-            if 0 <= t - n < count:
-                for half in (0, 1):
-                    stage(half, t - n)
-        if t == 0:
-            norm_start()
-            pack_own()
-        if t == 2:
-            norm_forward("y", 0)
-        if t == 3:
-            norm_middle()
-        if t == 5:
-            norm_forward("x", 4)
-        if t == 7:
-            norm_end()
+    stages = (begin, first_forward, second_send, update, share, share_forward, finish)
+    after = {0: (norm_start,), 1: (norm_middle, pack_own), 2: (norm_end,)}
+    for n, stage in enumerate(stages):
+        for s in range(len(SEGMENTS)):
+            for half in (0, 1):
+                stage(half, s)
+        for extra in after.get(n, ()):
+            extra()
     for copy in sent.values():
         copy.wait_send()
 
@@ -481,7 +432,7 @@
         down,
         mixed,
         mixed,
-        jax.ShapeDtypeStruct((1, 8 * LANES), BF16),
+        jax.ShapeDtypeStruct((8 * LANES,), BF16),
         jax.ShapeDtypeStruct((1, LANES // 2), F32),
         jax.ShapeDtypeStruct((1, LANES // 2), F32),
     )
@@ -492,7 +443,7 @@
     half_scratch = pltpu.VMEM((SIDE, SIDE, HALF_ROWS, LANES), BF16)
     part_scratch = pltpu.VMEM((SIDE, HALF_ROWS, LANES), BF16)
     from_1 = pltpu.VMEM((3, 2, SIDE, HALF_ROWS // 2, LANES), BF16)
-    from_2 = pltpu.VMEM((3, 2, HALF_ROWS // 2, LANES), BF16)
+    from_2 = pltpu.VMEM((3, HALF_ROWS, LANES), BF16)
     own = [pltpu.VMEM(s, F32) for s in shapes]
     own_packed = pltpu.VMEM((HALF_ROWS, LANES), F32)
     small = pltpu.VMEM((1, LANES // 2), F32)

time: 56.4 us -> 47.4 us (0.84)
  Pallas kernels: 55 us -> 46.6 us
  other arithmetic: 0.6 us -> 0 us
    pallas_call x1, Pallas kernels: 52.7 us -> 44.2 us  [body(): pl.pallas_call(exchange_kernel, out_shape=held, in_specs=[anywhere] * 21,...]
    pallas_call x1 -> x0, other arithmetic: 0.6 us -> none  [body(): pl.pallas_call(place_kernel, out_shape=(*tall, held[2], held[3], *own_row...]
where the time goes in v2:
time: 47.4 us; the launch traced here: 47.3 us
  Pallas kernels  46.6 us (98%)
  between operations  0.67 us (1%)
    pallas_call x1, Pallas kernels, body(): pl.pallas_call(exchange_kernel, out_shape=held, in_specs=[anywhere] * 21,...  44.2 us
    pallas_call x1, Pallas kernels, body(): pl.pallas_call(place_kernel, out_shape=(*tall, held[2], held[3], *own_row...  2.34 us

profile of v2, /device:TPU:0, one launch (start us, length us, event | category | flops | bytes accessed | tf_op | source)
XLA Modules:
  0.0 47.3 jit_solution(9798863225234309756)
XLA Ops:
  0.7 44.2 %exchange.1 = (bf16[4,4,384,128]{3,2,1,0:T(8,128)(2,1)S(1)}, bf16[4,4,384,128]{3,2,1,0:T(8,128)(2,1)S(1)}, bf16[512,1024]{1,0:T(8,128)(2,1)S(1)}, bf16[128,1024]...) custom-call(f32[1,1024,512]{2,1,0:T(8,128)} %refs_0_.1, ...), custom_call_target="tpu_custom_call" | custom-call | tf_op jit(solution)/shard_map/exchange/pallas_call | solution.py:450
  44.9 2.3 %place.1 = (bf16[4,4,64,512]{3,2,1,0:T(8,128)(2,1)}, bf16[4,4,64,128]{3,2,1,0:T(8,128)(2,1)}, bf16[4,4,64,128]{3,2,1,0:T(8,128)(2,1)}, bf16[4,4,64,128]{3,2,1,0:...) custom-call(bf16[4,4,384,128]{3,2,1,0:T(8,128)(2,1)S(1)} %get-tuple-, ...), custom_call_target="tpu_custom_call" | custom-call | tf_op jit(solution)/shard_map/place/pallas_call | solution.py:494

commit v3 on v2

--- a/solution.py
+++ b/solution.py
@@ -46,8 +46,8 @@
     return spans
 
 
-def count_remote():
-    return 2 * len(SEGMENTS) * 16 + 6
+SENT_GROUPS = 9
+ARRIVALS = 6
 
 
 def exchange_kernel(*refs):
@@ -87,12 +87,15 @@
         at[axis] = step[axis][d]
         return {"batch": at["y"] * SIDE + at["x"]}
 
-    loads = {}
-
-    def load(key, source, target):
-        copy = pltpu.make_async_copy(source, target, load_sem.at[len(loads)])
-        copy.start()
-        loads[key] = copy
+
+    def load(group, source, target):
+        pltpu.make_async_copy(source, target, load_sem.at[group]).start()
+
+    def loaded(group, size_of):
+        pltpu.make_async_copy(size_of, size_of, load_sem.at[group]).wait()
+
+    own_loads = 2 * len(SEGMENTS)
+    norm_loads = ((grad_norm, norm_grad_in), (weight_norm, norm_weight_in), (moment_norm, norm_moment_in))
 
     def load_segment(half, s):
         at, count = segment_spans()[s]
@@ -100,17 +103,16 @@
             name, part_no = PIECES[half][k]
             lanes = pl.ds(part_no * LANES, LANES)
             if name in ROW_CUT:
-                load((half, k), grad[name].at[0, :, lanes], landed[0].at[slot_of(half, k)])
+                load(half * len(SEGMENTS) + s, grad[name].at[0, :, lanes], landed[0].at[slot_of(half, k)])
             else:
-                load((half, k), grad[name].at[0, lanes, :], landed[1].at[slot_of(half, k)])
+                load(half * len(SEGMENTS) + s, grad[name].at[0, lanes, :], landed[1].at[slot_of(half, k)])
 
     def load_own():
-        load("norm_grad", grad_norm, norm_grad_in)
-        load("norm_weight", weight_norm, norm_weight_in)
-        load("norm_moment", moment_norm, norm_moment_in)
+        for n, (source, target) in enumerate(norm_loads):
+            load(own_loads + 1 + n, source, target)
         for name in NAMES:
-            load(("weight", name), weight[name], weight_in[name])
-            load(("moment", name), moment[name], moment_in[name])
+            load(own_loads, weight[name], weight_in[name])
+            load(own_loads, moment[name], moment_in[name])
 
     for half in (0, 1):
         load_segment(half, 0)
@@ -121,7 +123,6 @@
 
     def pack_piece(half, k):
         name, part_no = PIECES[half][k]
-        loads[half, k].wait()
         rows = pl.ds(k * ROWS, ROWS)
         slot = slot_of(half, k)
 
@@ -141,12 +142,10 @@
                 put(2 * m + 1, pair[1])
 
     def pack_own():
+        loaded(own_loads, landed[0].at[0:3, 0 : SIDE * SIDE * ROWS // 2, :])
         for half in (0, 1):
             for k, (name, part_no) in enumerate(PIECES[half]):
                 rows = pl.ds(k * ROWS, ROWS)
-                if part_no == 0:
-                    loads["weight", name].wait()
-                    loads["moment", name].wait()
                 for source, target in ((weight_in[name], weight_packed[half]), (moment_in[name], moment_packed[half])):
                     if name in ROW_CUT:
                         target[rows, :] = source[:, part_no * LANES : (part_no + 1) * LANES]
@@ -154,23 +153,26 @@
                         turned = source[:, part_no * LANES : (part_no + 1) * LANES].T
                         target[rows, :] = jnp.concatenate([turned[:ROWS, :], turned[ROWS:, :]], axis=1)
 
-    sent = {}
-
-    def send(key, source, target, axis, d):
-        n = len(sent)
-        copy = pltpu.make_async_remote_copy(
+    def remote(source, target, axis, d, group, slot):
+        return pltpu.make_async_remote_copy(
             src_ref=source,
             dst_ref=target,
-            send_sem=send_sem.at[n],
-            recv_sem=recv_sem.at[n],
+            send_sem=send_sem.at[group],
+            recv_sem=recv_sem.at[slot],
             device_id=device(axis, d),
             device_id_type=pl.DeviceIdType.MESH,
         )
-        copy.start()
-        sent[key] = copy
-
-    def arrived(key):
-        sent[key].wait_recv()
+
+    def slot_at(half, s, kind):
+        return (half * len(SEGMENTS) + s) * ARRIVALS + kind
+
+    norm_slots = {"y": slot_at(2, 0, 0), "x": slot_at(2, 0, 1)}
+
+    def arrived(slot, size_of):
+        remote(size_of, size_of, "y", 1, 0, slot).wait_recv()
+
+    def all_sent(group, size_of):
+        remote(size_of, size_of, "y", 1, group, 0).wait_send()
 
     def spans(s):
         at, count = segment_spans()[s]
@@ -181,28 +183,31 @@
         axis = AXES[half][0]
         low, high, place, _ = spans(s)
         data, land = packed[half], from_1[half]
-        send((half, s, 0, 1), data.at[step[axis][2], :, low, :], land.at[0, 0, :, place, :], axis, 1)
-        send((half, s, 0, -1), data.at[step[axis][2], :, high, :], land.at[0, 1, :, place, :], axis, -1)
-        send((half, s, 1, 1), data.at[step[axis][1], :, high, :], land.at[1, 0, :, place, :], axis, 1)
-        send((half, s, 1, -1), data.at[step[axis][-1], :, low, :], land.at[1, 1, :, place, :], axis, -1)
+        group, near, far = half * 4, slot_at(half, s, 0), slot_at(half, s, 1)
+        for source, rows, kind, side, d, slot in (
+            (2, low, 0, 0, 1, near),
+            (2, high, 0, 1, -1, near),
+            (1, high, 1, 0, 1, far),
+            (-1, low, 1, 1, -1, far),
+        ):
+            remote(data.at[step[axis][source], :, rows, :], land.at[kind, side, :, place, :], axis, d, group, slot).start()
 
     def first_forward(half, s):
         axis = AXES[half][0]
         low, high, place, _ = spans(s)
         data, land = packed[half], from_1[half]
+        arrived(slot_at(half, s, 0), land.at[0, :, :, place, :])
         for side, d, rows in ((0, 1, low), (1, -1, high)):
-            arrived((half, s, 0, d))
             to = step[axis][d]
             total = data[to, :, rows, :].astype(F32) + land[0, side, :, place, :].astype(F32)
             data[to, :, rows, :] = total.astype(BF16)
-            send((half, s, 2, d), data.at[to, :, rows, :], land.at[2, side, :, place, :], axis, d)
+            target = land.at[2, side, :, place, :]
+            remote(data.at[to, :, rows, :], target, axis, d, half * 4, slot_at(half, s, 1)).start()
 
     def second_send(half, s):
         low, high, place, whole = spans(s)
         data, land = packed[half], from_1[half]
-        for kind in (1, 2):
-            for d in (1, -1):
-                arrived((half, s, kind, d))
+        arrived(slot_at(half, s, 1), land.at[1:3, :, :, place, :])
         mine = here[AXES[half][0]]
         for rows, first, second in ((low, 2, 1), (high, 1, 2)):
             total = data[mine, :, rows, :].astype(F32)
@@ -211,15 +216,15 @@
             part[half][:, rows, :] = total.astype(BF16)
         axis = AXES[half][1]
         for n, d in ((2, 2), (0, 1), (1, -1)):
-            send((half, s, 3, d), part[half].at[step[axis][d], whole, :], from_2[half].at[n, whole, :], axis, d)
+            source, target = part[half].at[step[axis][d], whole, :], from_2[half].at[n, whole, :]
+            remote(source, target, axis, d, half * 4 + 1, slot_at(half, s, 2)).start()
 
     mean_rate = float(SIDE * SIDE) ** -0.5
 
     def update(half, s):
         first, second = AXES[half]
         whole = spans(s)[3]
-        for d in AWAY:
-            arrived((half, s, 3, d))
+        arrived(slot_at(half, s, 2), from_2[half].at[:, whole, :])
         total = part[half][here[second], whole, :].astype(F32)
         for n in range(3):
             total += from_2[half][n, whole, :].astype(F32)
@@ -230,7 +235,7 @@
         full[half][here[first], here[second], whole, :] = new.astype(BF16)
         own = full[half].at[here[first], here[second], whole, :]
         for d in (2, 1, -1):
-            send((half, s, 4, d), own, own, second, d)
+            remote(own, own, second, d, half * 4 + 2, slot_at(half, s, 3)).start()
 
     def turn_own(half, s):
         at, count = segment_spans()[s]
@@ -245,21 +250,21 @@
                 target[:, part_no * LANES : (part_no + 1) * LANES] = jnp.concatenate([turned[:ROWS, :], turned[ROWS:, :]], axis=1)
 
     def share(half, s):
-        for d in AWAY:
-            arrived((half, s, 4, d))
+        whole = spans(s)[3]
+        arrived(slot_at(half, s, 3), full[half].at[0, 0:3, whole, :])
         first = AXES[half][0]
-        block = full[half].at[here[first], :, spans(s)[3], :]
+        block = full[half].at[here[first], :, whole, :]
         for d in (1, -1):
-            send((half, s, 5, d), block, block, first, d)
+            remote(block, block, first, d, half * 4 + 3, slot_at(half, s, 4)).start()
         turn_own(half, s)
 
     def share_forward(half, s):
         first = AXES[half][0]
-        low, high, _, _ = spans(s)
+        low, high, _, whole = spans(s)
+        arrived(slot_at(half, s, 4), full[half].at[0:2, :, whole, :])
         for d, rows in ((1, low), (-1, high)):
-            arrived((half, s, 5, d))
             block = full[half].at[step[first][-d], :, rows, :]
-            send((half, s, 6, d), block, block, first, d)
+            remote(block, block, first, d, half * 4 + 3, slot_at(half, s, 5)).start()
 
     def unpack(half, s):
         at, count = segment_spans()[s]
@@ -281,8 +286,8 @@
                 target[part_no * LANES + ROWS : (part_no + 1) * LANES, lanes] = bottom.astype(BF16)
 
     def norm_start():
-        for key in ("norm_grad", "norm_weight", "norm_moment"):
-            loads[key].wait()
+        for n, (_, target) in enumerate(norm_loads):
+            loaded(own_loads + 1 + n, target)
         for k in range(8):
             norm_tiles[0, k : k + 1, :] = norm_grad_in[0:1, k * LANES : (k + 1) * LANES]
         base = norm_weight_in[...] - learn_rate * (hold_rate * norm_moment_in[...])
@@ -294,11 +299,10 @@
 
     def norm_send(axis, at):
         for n, d in enumerate(AWAY):
-            send(("norm", axis, d), norm_tiles.at[at], norm_tiles.at[at + 1 + n], axis, d)
+            remote(norm_tiles.at[at], norm_tiles.at[at + 1 + n], axis, d, 8, norm_slots[axis]).start()
 
     def norm_total(axis, at):
-        for d in AWAY:
-            arrived(("norm", axis, d))
+        arrived(norm_slots[axis], norm_tiles.at[at + 1 : at + 4])
         return (norm_tiles[at] + norm_tiles[at + 1]) + (norm_tiles[at + 2] + norm_tiles[at + 3])
 
     def norm_middle():
@@ -320,6 +324,7 @@
 
     def begin(half, s):
         at, count = segment_spans()[s]
+        loaded(half * len(SEGMENTS) + s, landed[0].at[0:count])
         for k in range(at, at + count):
             pack_piece(half, k)
         if half == 0 and s == 0:
@@ -331,8 +336,7 @@
             load_own()
 
     def finish(half, s):
-        for d in (1, -1):
-            arrived((half, s, 6, d))
+        arrived(slot_at(half, s, 5), full[half].at[0, :, spans(s)[3], :])
         unpack(half, s)
 
     stages = (begin, first_forward, second_send, update, share, share_forward, finish)
@@ -343,8 +347,10 @@
                 stage(half, s)
         for extra in after.get(n, ()):
             extra()
-    for copy in sent.values():
-        copy.wait_send()
+    for half in (0, 1):
+        for n, size_of in enumerate((from_1[half], from_2[half], from_2[half], from_1[half])):
+            all_sent(half * 4 + n, size_of)
+    all_sent(8, norm_tiles.at[0:6])
 
 
 def slot_of(half, k):
@@ -375,11 +381,9 @@
     norms_out = take(3)
     (sem,) = take(1)
     assert not refs
-    copies = []
-
-    def put(source, target):
-        copies.append(pltpu.make_async_copy(source, target, sem.at[len(copies)]))
-        copies[-1].start()
+
+    def put(source, target, group):
+        pltpu.make_async_copy(source, target, sem.at[group]).start()
 
     for half in (0, 1):
         for k, (name, part_no) in enumerate(PIECES[half]):
@@ -387,25 +391,22 @@
                 continue
             rows, lanes = pl.ds(k * ROWS, ROWS), pl.ds(part_no * LANES, LANES)
             if AXES[half][0] == "y":
-                put(full[half].at[:, :, rows, :], copy_out[name].at[:, :, :, lanes])
+                put(full[half].at[:, :, rows, :], copy_out[name].at[:, :, :, lanes], 0)
             else:
                 for n in range(SIDE):
-                    put(full[half].at[n, :, rows, :], copy_out[name].at[:, n, :, lanes])
-            put(new_rows[half].at[rows, :], new_out[name].at[:, lanes])
-            put(state_rows[half].at[rows, :], state_out[name].at[:, lanes])
-    put(full_down, copy_down)
-    put(full_mixed, copy_mixed)
-    put(new_down_in, new_down)
-    put(state_down_in, state_down)
-    put(new_mixed_in, new_mixed)
-    put(state_mixed_in, state_mixed)
-    for source, target in zip(norms_in, norms_out):
-        put(source, target)
-    for copy in copies:
-        copy.wait()
-
-
-PLACE_COPIES = 2 + 4 + 6 * 2 + 4 + 4 + 2 * 7 + 3
+                    put(full[half].at[n, :, rows, :], copy_out[name].at[:, n, :, lanes], 1)
+            put(new_rows[half].at[rows, :], new_out[name].at[:, lanes], 2)
+            put(state_rows[half].at[rows, :], state_out[name].at[:, lanes], 2)
+    put(full_down, copy_down, 1)
+    put(full_mixed, copy_mixed, 1)
+    put(new_down_in, new_down, 2)
+    put(state_down_in, state_down, 2)
+    put(new_mixed_in, new_mixed, 2)
+    put(state_mixed_in, state_mixed, 2)
+    for n, (source, target) in enumerate(zip(norms_in, norms_out)):
+        put(source, target, 3 + n)
+    for group, size_of in enumerate((full[0], full[1], full[0].at[0:2], *norms_in)):
+        pltpu.make_async_copy(size_of, size_of, sem.at[group]).wait()
 
 
 def in_hbm(arrays):
@@ -437,7 +438,7 @@
         jax.ShapeDtypeStruct((1, LANES // 2), F32),
     )
     dma = pltpu.SemaphoreType.DMA
-    remote = count_remote()
+    remote = 2 * len(SEGMENTS) * ARRIVALS + 2
     vmem = pl.BlockSpec(memory_space=pltpu.VMEM)
     anywhere = pl.BlockSpec(memory_space=pltpu.HBM)
     half_scratch = pltpu.VMEM((SIDE, SIDE, HALF_ROWS, LANES), BF16)
@@ -473,8 +474,8 @@
             small,
             small,
             pltpu.VMEM((9, 16, LANES), F32),
-            dma((27,)),
-            dma((remote,)),
+            dma((2 * len(SEGMENTS) + 4,)),
+            dma((SENT_GROUPS,)),
             dma((remote,)),
         ],
         compiler_params=pltpu.CompilerParams(
@@ -496,7 +497,7 @@
         out_shape=(*tall, held[2], held[3], *own_rows, down, mixed, *own_rows, down, mixed, *held[12:]),
         in_specs=[vmem] * 15,
         out_specs=[anywhere] * 21,
-        scratch_shapes=[dma((PLACE_COPIES,))],
+        scratch_shapes=[dma((6,))],
         compiler_params=pltpu.CompilerParams(vmem_limit_bytes=16 * 1024 * 1024),
         name="place",
     )(*results)

time: 47.4 us -> 45.6 us (0.962)
  Pallas kernels: 46.6 us -> 44.8 us
    pallas_call x1, Pallas kernels: 44.2 us -> 42.8 us  [body(): pl.pallas_call(exchange_kernel, out_shape=held, in_specs=[anywhere] * 21,...]
where the time goes in v3:
time: 45.6 us; the launch traced here: 45.4 us
  Pallas kernels  44.8 us (98%)
  between operations  0.67 us (1%)
    pallas_call x1, Pallas kernels, body(): pl.pallas_call(exchange_kernel, out_shape=held, in_specs=[anywhere] * 21,...  42.8 us
    pallas_call x1, Pallas kernels, body(): pl.pallas_call(place_kernel, out_shape=(*tall, held[2], held[3], *own_row...  2.01 us

profile of v3, /device:TPU:0, one launch (start us, length us, event | category | flops | bytes accessed | tf_op | source)
XLA Modules:
  0.0 45.4 jit_solution(2654846251426059118)
XLA Ops:
  0.7 42.8 %exchange.1 = (bf16[4,4,384,128]{3,2,1,0:T(8,128)(2,1)S(1)}, bf16[4,4,384,128]{3,2,1,0:T(8,128)(2,1)S(1)}, bf16[512,1024]{1,0:T(8,128)(2,1)S(1)}, bf16[128,1024]...) custom-call(f32[1,1024,512]{2,1,0:T(8,128)} %refs_0_.1, ...), custom_call_target="tpu_custom_call" | custom-call | tf_op jit(solution)/shard_map/exchange/pallas_call | solution.py:451
  43.4 2.0 %place.1 = (bf16[4,4,64,512]{3,2,1,0:T(8,128)(2,1)}, bf16[4,4,64,128]{3,2,1,0:T(8,128)(2,1)}, bf16[4,4,64,128]{3,2,1,0:T(8,128)(2,1)}, bf16[4,4,64,128]{3,2,1,0:...) custom-call(bf16[4,4,384,128]{3,2,1,0:T(8,128)(2,1)S(1)} %get-tuple-, ...), custom_call_target="tpu_custom_call" | custom-call | tf_op jit(solution)/shard_map/place/pallas_call | solution.py:495

commit v4 on v3

--- a/solution.py
+++ b/solution.py
@@ -20,6 +20,9 @@
 )
 SEGMENTS = (2, 3, 1)
 HALF_ROWS = ROWS * 6
+REDUCE = ("B0", "B1", "B2", "N", "F0", "F1", "F2", "M", "O", "T0", "T1", "T2", "X")
+GATHER_FAR = ("U0", "U1", "U2", "S0", "S1", "S2", "G0", "G1", "G2", "E0", "E1", "E2")
+GATHER_NEAR = ("U0", "U1", "U2", "S0", "S1", "S2", "L0", "L1", "L2", "G0", "G1", "G2", "E0", "E1", "E2")
 AXES = (("y", "x"), ("x", "y"))
 AWAY = (1, -1, 2)
 F32, BF16 = jnp.float32, jnp.bfloat16
@@ -47,7 +50,7 @@
 
 
 SENT_GROUPS = 9
-ARRIVALS = 6
+ARRIVALS = 7
 
 
 def exchange_kernel(*refs):
@@ -221,7 +224,7 @@
 
     mean_rate = float(SIDE * SIDE) ** -0.5
 
-    def update(half, s):
+    def update(half, s, far):
         first, second = AXES[half]
         whole = spans(s)[3]
         arrived(slot_at(half, s, 2), from_2[half].at[:, whole, :])
@@ -234,8 +237,10 @@
         new_rows[half][whole, :] = new
         full[half][here[first], here[second], whole, :] = new.astype(BF16)
         own = full[half].at[here[first], here[second], whole, :]
-        for d in (2, 1, -1):
+        for d in (2, 1, -1) if far else (1, -1):
             remote(own, own, second, d, half * 4 + 2, slot_at(half, s, 3)).start()
+        if not far:
+            share_block(half, s, 0)
 
     def turn_own(half, s):
         at, count = segment_spans()[s]
@@ -249,22 +254,44 @@
                 turned = source[rows, :].T
                 target[:, part_no * LANES : (part_no + 1) * LANES] = jnp.concatenate([turned[:ROWS, :], turned[ROWS:, :]], axis=1)
 
-    def share(half, s):
+    def share_block(half, s, away):
+        first, second = AXES[half]
+        at = step[second][away] if away else here[second]
+        block = full[half].at[here[first], at, spans(s)[3], :]
+        for d in (1, -1):
+            remote(block, block, first, d, half * 4 + 3, slot_at(half, s, 5)).start()
+
+    def share_all(half, s):
+        first = AXES[half][0]
         whole = spans(s)[3]
         arrived(slot_at(half, s, 3), full[half].at[0, 0:3, whole, :])
-        first = AXES[half][0]
         block = full[half].at[here[first], :, whole, :]
         for d in (1, -1):
-            remote(block, block, first, d, half * 4 + 3, slot_at(half, s, 4)).start()
+            remote(block, block, first, d, half * 4 + 3, slot_at(half, s, 5)).start()
         turn_own(half, s)
+
+    def share(half, s):
+        first, second = AXES[half]
+        low, high, _, whole = spans(s)
+        arrived(slot_at(half, s, 3), full[half].at[0, 0:2, whole, :])
+        for d, rows in ((1, low), (-1, high)):
+            block = full[half].at[here[first], step[second][-d], rows, :]
+            remote(block, block, second, d, half * 4 + 2, slot_at(half, s, 4)).start()
+        for away in (1, -1):
+            share_block(half, s, away)
+        turn_own(half, s)
+
+    def share_last(half, s):
+        arrived(slot_at(half, s, 4), full[half].at[0, 0, spans(s)[3], :])
+        share_block(half, s, 2)
 
     def share_forward(half, s):
         first = AXES[half][0]
         low, high, _, whole = spans(s)
-        arrived(slot_at(half, s, 4), full[half].at[0:2, :, whole, :])
+        arrived(slot_at(half, s, 5), full[half].at[0:2, :, whole, :])
         for d, rows in ((1, low), (-1, high)):
             block = full[half].at[step[first][-d], :, rows, :]
-            remote(block, block, first, d, half * 4 + 3, slot_at(half, s, 5)).start()
+            remote(block, block, first, d, half * 4 + 3, slot_at(half, s, 6)).start()
 
     def unpack(half, s):
         at, count = segment_spans()[s]
@@ -336,17 +363,32 @@
             load_own()
 
     def finish(half, s):
-        arrived(slot_at(half, s, 5), full[half].at[0, :, spans(s)[3], :])
+        arrived(slot_at(half, s, 6), full[half].at[0, :, spans(s)[3], :])
         unpack(half, s)
 
-    stages = (begin, first_forward, second_send, update, share, share_forward, finish)
-    after = {0: (norm_start,), 1: (norm_middle, pack_own), 2: (norm_end,)}
-    for n, stage in enumerate(stages):
-        for s in range(len(SEGMENTS)):
-            for half in (0, 1):
-                stage(half, s)
-        for extra in after.get(n, ()):
-            extra()
+    def run(order, far=False):
+        stages = dict(
+            B=begin,
+            F=first_forward,
+            T=second_send,
+            U=lambda half, s: update(half, s, far),
+            S=share_all if far else share,
+            L=share_last,
+            G=share_forward,
+            E=finish,
+        )
+        extras = dict(N=norm_start, M=norm_middle, O=pack_own, X=norm_end)
+        for name in order:
+            if name in extras:
+                extras[name]()
+            else:
+                for half in (0, 1):
+                    stages[name[0]](half, int(name[1]))
+
+    run(REDUCE)
+    core = lax.rem(lax.axis_index("cols"), 2)
+    pl.when(core == 0)(lambda: run(GATHER_FAR, far=True))
+    pl.when(core == 1)(lambda: run(GATHER_NEAR))
     for half in (0, 1):
         for n, size_of in enumerate((from_1[half], from_2[half], from_2[half], from_1[half])):
             all_sent(half * 4 + n, size_of)

time: 45.6 us -> 44.4 us (0.974)
  Pallas kernels: 44.8 us -> 43.6 us
    pallas_call x1, Pallas kernels: 42.8 us -> 41.6 us  [body(): pl.pallas_call(exchange_kernel, out_shape=held, in_specs=[anywhere] * 21,...]
where the time goes in v4:
time: 44.4 us; the launch traced here: 44.3 us
  Pallas kernels  43.6 us (98%)
  between operations  0.67 us (2%)
    pallas_call x1, Pallas kernels, body(): pl.pallas_call(exchange_kernel, out_shape=held, in_specs=[anywhere] * 21,...  41.6 us
    pallas_call x1, Pallas kernels, body(): pl.pallas_call(place_kernel, out_shape=(*tall, held[2], held[3], *own_row...  2.01 us

profile of v4, /device:TPU:0, one launch (start us, length us, event | category | flops | bytes accessed | tf_op | source)
XLA Modules:
  0.0 44.3 jit_solution(5078094207169607002)
XLA Ops:
  0.7 41.6 %exchange.1 = (bf16[4,4,384,128]{3,2,1,0:T(8,128)(2,1)S(1)}, bf16[4,4,384,128]{3,2,1,0:T(8,128)(2,1)S(1)}, bf16[512,1024]{1,0:T(8,128)(2,1)S(1)}, bf16[128,1024]...) custom-call(f32[1,1024,512]{2,1,0:T(8,128)} %refs_0_.1, ...), custom_call_target="tpu_custom_call" | custom-call | tf_op jit(solution)/shard_map/exchange/pallas_call | solution.py:493
  42.2 2.0 %place.1 = (bf16[4,4,64,512]{3,2,1,0:T(8,128)(2,1)}, bf16[4,4,64,128]{3,2,1,0:T(8,128)(2,1)}, bf16[4,4,64,128]{3,2,1,0:T(8,128)(2,1)}, bf16[4,4,64,128]{3,2,1,0:...) custom-call(bf16[4,4,384,128]{3,2,1,0:T(8,128)(2,1)S(1)} %get-tuple-, ...), custom_call_target="tpu_custom_call" | custom-call | tf_op jit(solution)/shard_map/place/pallas_call | solution.py:537

commit v5 on v4

--- a/solution.py
+++ b/solution.py
@@ -20,9 +20,9 @@
 )
 SEGMENTS = (2, 3, 1)
 HALF_ROWS = ROWS * 6
-REDUCE = ("B0", "B1", "B2", "N", "F0", "F1", "F2", "M", "O", "T0", "T1", "T2", "X")
-GATHER_FAR = ("U0", "U1", "U2", "S0", "S1", "S2", "G0", "G1", "G2", "E0", "E1", "E2")
-GATHER_NEAR = ("U0", "U1", "U2", "S0", "S1", "S2", "L0", "L1", "L2", "G0", "G1", "G2", "E0", "E1", "E2")
+REDUCE = ("B0", "B1", "B2", "F0", "N", "F1", "F2", "O", "T0", "T1", "M", "T2")
+GATHER_FAR = ("U0", "U1", "U2", "X", "S0", "S1", "S2", "G0", "G1", "G2", "E0", "E1", "E2")
+GATHER_NEAR = ("U0", "U1", "U2", "X", "S0", "S1", "S2", "L0", "L1", "L2", "G0", "G1", "G2", "E0", "E1", "E2")
 AXES = (("y", "x"), ("x", "y"))
 AWAY = (1, -1, 2)
 F32, BF16 = jnp.float32, jnp.bfloat16
@@ -121,7 +121,7 @@
         load_segment(half, 0)
     barrier = pltpu.get_barrier_semaphore()
     for axis in ("y", "x"):
-        for d in AWAY:
+        for d in (1, -1):
             pl.semaphore_signal(barrier, inc=1, device_id=device(axis, d), device_id_type=pl.DeviceIdType.MESH)
 
     def pack_piece(half, k):
@@ -355,7 +355,7 @@
         for k in range(at, at + count):
             pack_piece(half, k)
         if half == 0 and s == 0:
-            pl.semaphore_wait(barrier, 2 * len(AWAY))
+            pl.semaphore_wait(barrier, 4)
         first_send(half, s)
         if s + 1 < len(SEGMENTS):
             load_segment(half, s + 1)

time: 44.4 us -> 44.2 us (level)
  no operation moved by 1% of the time
where the time goes in v5:
time: 44.2 us; the launch traced here: 44 us
  Pallas kernels  43.3 us (98%)
  between operations  0.67 us (2%)
    pallas_call x1, Pallas kernels, body(): pl.pallas_call(exchange_kernel, out_shape=held, in_specs=[anywhere] * 21,...  41.3 us
    pallas_call x1, Pallas kernels, body(): pl.pallas_call(place_kernel, out_shape=(*tall, held[2], held[3], *own_row...  2.01 us

profile of v5, /device:TPU:0, one launch (start us, length us, event | category | flops | bytes accessed | tf_op | source)
XLA Modules:
  0.0 44.0 jit_solution(6333435468454903084)
XLA Ops:
  0.7 41.3 %exchange.1 = (bf16[4,4,384,128]{3,2,1,0:T(8,128)(2,1)S(1)}, bf16[4,4,384,128]{3,2,1,0:T(8,128)(2,1)S(1)}, bf16[512,1024]{1,0:T(8,128)(2,1)S(1)}, bf16[128,1024]...) custom-call(f32[1,1024,512]{2,1,0:T(8,128)} %refs_0_.1, ...), custom_call_target="tpu_custom_call" | custom-call | tf_op jit(solution)/shard_map/exchange/pallas_call | solution.py:493
  42.0 2.0 %place.1 = (bf16[4,4,64,512]{3,2,1,0:T(8,128)(2,1)}, bf16[4,4,64,128]{3,2,1,0:T(8,128)(2,1)}, bf16[4,4,64,128]{3,2,1,0:T(8,128)(2,1)}, bf16[4,4,64,128]{3,2,1,0:...) custom-call(bf16[4,4,384,128]{3,2,1,0:T(8,128)(2,1)S(1)} %get-tuple-, ...), custom_call_target="tpu_custom_call" | custom-call | tf_op jit(solution)/shard_map/place/pallas_call | solution.py:537
